TPU v7x, 128 devices: a whole 4x4x4 slice. The times are simulated.
128 devices in a mesh: gx: 8 (over x, core), gy: 16 (over y, z).
Axes of the slice: x: 4, y: 4, z: 4, core: 2. Of those that a mesh axis runs over, the one named last changes fastest.
Arguments:
- state: float32 [32, 768, 2048], P('gx', None, 'gy'), may hold values from -6 to 6
- forcing: float32 [32, 768, 2048], P('gx', None, 'gy'), may hold values from -6 to 6
- vertical_mix: float32 [768, 768], replicated, may hold values from -0.21875 to 0.21875
- diffusion: float32 [768], replicated, may hold values from 0.1 to 1
- column_class: int32 [32, 2048], P('gx', 'gy'), may hold values from 0 to 2
- block_regime: int32 [16, 32, 1], P('gy', 'gx'), may hold values from 0 to 7; in each aligned block of 4 rows (0 to 3, 4 to 7, ..., all dimensions but the last counted through in order) no two rows name the same one
- correction_ops: float32 [8, 768, 768], P('gx'), may hold values from -0.21875 to 0.21875
Outputs:
- new_state: float32 [32, 768, 2048], P('gx', None, 'gy')
Inputs may be any that keep to these rules, and one draw needn't show every extreme that they name: `block_regime`: among the blocks of one device (the same first index, 4 consecutive grid rows) no regime appears twice.
All inputs are finite; a program needn't handle non-finite values.
Results may differ from a plain program's by a relative error of at most 0.0002.
Values sent between devices are 32-bit elements; how exact they have to be, the bound alone decides.
No kernel may reach another device: no remote copies, remote signals or barrier semaphores. Data moves between devices by JAX's collectives and lax.ppermute only.
A program may use at most 128 MiB of HBM per device.

v0:
```python
import functools
import jax
import jax.numpy as jnp
from jax import lax
from jax.sharding import Mesh
from jax.sharding import PartitionSpec as P

ITERS = 4
GX_GY = ("gx_0", "gx_1", "gy_0", "gy_1")
GX = ("gx_0", "gx_1")
GY = ("gy_0", "gy_1")


def one_axis_at_a_time(array, axes):
    return functools.reduce(lax.psum, axes, array)


def padded_2(array, sides, width):
    edges = {}
    for axis, dim in sides:
        devices, length = (lax.axis_size(axis), array.shape[dim])
        up = [(i, (i + 1) % devices) for i in range(devices - 1)]
        last = lax.slice_in_dim(array, length - width, length, axis=dim)
        first = lax.slice_in_dim(array, 0, width, axis=dim)
        edges[dim] = (
            lax.ppermute(last, axis, up),
            lax.ppermute(first, axis, [(b, a) for a, b in up]),
        )
    done = []
    for _, dim in sides:
        low, high = edges[dim]
        around = [(width, width) if d in done else (0, 0) for d in range(array.ndim)]
        array = jnp.concatenate([jnp.pad(low, around), array, jnp.pad(high, around)], axis=dim)
        done.append(dim)
    return array


def squares(field):
    return one_axis_at_a_time(jnp.sum(field * field), GX_GY)


def chol_solve(factor, target):
    count = target.shape[0]
    forward = []
    for index in range(count):
        value = target[index]
        for other in range(index):
            value = value - factor[index, other] * forward[other]
        forward.append(value / factor[index, index])
    backward = [None] * count
    for index in range(count - 1, -1, -1):
        value = forward[index]
        for other in range(index + 1, count):
            value = value - factor[other, index] * backward[other]
        backward[index] = value / factor[index, index]
    return jnp.stack(backward)


def local(state, forcing, vertical_mix, diffusion, column_class, block_regime, correction_ops):
    highest = lax.Precision.HIGHEST
    regimes = block_regime[0, :, 0]
    weights = (column_class.astype(jnp.float32) * 0.5)[:, None, :]
    coeff_rows = diffusion[None, :, None]

    def spread(field):
        padded = padded_2(field, ((GX, 0), (GY, 2)), 1)
        centre = padded[1:-1, :, 1:-1]
        lap = (
            4.0 * centre
            - padded[2:, :, 1:-1]
            - padded[:-2, :, 1:-1]
            - padded[1:-1, :, 2:]
            - padded[1:-1, :, :-2]
        )
        mixed = jnp.einsum("pq,xqy->xpy", vertical_mix, field, precision=highest)
        return 2.0 * field + mixed + coeff_rows * lap

    every_op = lax.all_gather(correction_ops, GX, axis=0, tiled=True)
    chosen = every_op[regimes]

    def correct(field):
        return jnp.einsum("bpq,bqc->bpc", chosen, field, precision=highest) * weights

    shade = jnp.tanh(state)
    slope = 1.0 - shade * shade
    residual = forcing - (spread(state) + correct(shade))
    beta = jnp.sqrt(squares(residual) + 1e-12)
    basis = [residual / beta]
    columns = []
    for step in range(ITERS):
        current = basis[-1]
        image = spread(current) + correct(slope * current)
        locals_sum = jnp.stack([jnp.sum(vector * image) for vector in basis])
        coefs = one_axis_at_a_time(locals_sum, GX_GY)
        for index in range(len(basis)):
            image = image - coefs[index] * basis[index]
        length = jnp.sqrt(squares(image) + 1e-12)
        column = jnp.concatenate([coefs, length[None], jnp.zeros((ITERS - step - 1,), jnp.float32)])
        columns.append(column)
        if step + 1 < ITERS:
            basis.append(image / length)
    hess = jnp.stack(columns, axis=1)
    gram = jnp.dot(hess.T, hess, precision=highest)
    target = beta * hess[0]
    factor = jnp.linalg.cholesky(gram)
    solved = chol_solve(factor, target)
    new_state = state
    for index in range(ITERS):
        new_state = new_state + solved[index] * basis[index]
    return new_state


def solution(mesh):
    finer = Mesh(mesh.devices.reshape(4, 2, 4, 4), ("gx_0", "gx_1", "gy_0", "gy_1"))
    in_specs = (
        P(GX, None, GY),
        P(GX, None, GY),
        P(),
        P(),
        P(GX, GY),
        P(GY, GX, None),
        P(GX, None, None),
    )
    out_specs = P(GX, None, GY)
    return jax.shard_map(local, mesh=finer, in_specs=in_specs, out_specs=out_specs, check_vma=False)
```

profile of v0, /device:TPU:34, one launch (start us, length us, event | category | flops | bytes accessed | tf_op | source)
XLA Modules:
  0.0 631.4 jit_solution(1450121057735657620)
XLA Ops:
  27.3 81.3 %all-gather.2.cloned.1.call-done = f32[8,768,768]{2,1,0:T(8,128)} async-done(((f32[1,768,768]{2,1,0:T(8,128)}), f32[8,768,768]{2,1,0:T(8,128)}) %all-gather.2.cloned.1.call-update) | async-done | bytes 18874384 | tf_op jit(solution)/shard_map/all_gather | solution.py:78
  108.7 11.2 %gather_fusion = f32[4,768,768]{2,1,0:T(8,128)} fusion(f32[8,768,768]{2,1,0:T(8,128)} %all-gather.2.cloned.1.call-done, s32[1024]{0:T(1024)S(1)} %pad_clamp_fusion), kind=kCustom, calls=%fused_computation | custom fusion | bytes 18874384 | tf_op jit(solution)/shard_map/gather | solution.py:79
  119.9 13.6 %fusion.74 = f32[4,768,128]{1,2,0:T(8,128)S(1)} fusion(f32[4,768,768]{2,1,0:T(8,128)} %gather_fusion, f32[4,768,128]{1,2,0:T(8,128)} %copy.40), kind=kOutput, calls=%fused_computation.132 | convolution fusion | flops 3623878656 | bytes 12582912 | tf_op jit(solution)/shard_map/bpq,bqc->bpc/dot_general | solution.py:82
  133.7 11.4 %multiply_reduce_fusion.14 = (f32[]{:T(128)}, f32[4,768,128]{1,2,0:T(8,128)}) fusion(f32[4,768,128]{1,2,0:T(8,128)S(1)} %copy-done.16, f32[4,768,128]{1,2,0:T(8,128)S(1)} %fusion.74, f32[4,128]{1,0:T(4,128)S(1)} %convert_multiply_fusion, f32[1,768,128]{1,2,0:T(8,128)} %collective-permute-done, f32[4,768,128]{1,2,0:T(8,128)S(1)} %copy-done.1, ...), kind=kOutput, calls=%fused_computation.131 | convolution fusion | flops 3634888704 | bytes 11039748 | tf_op jit(solution)/shard_map/pq,xqy->xpy/dot_general | solution.py:75
  145.0 8.9 %psum.252 = f32[]{:T(128)} all-reduce(f32[]{:T(128)} %get-tuple-element.61), channel_id=1, replica_groups=mesh['gx_0'=4,'gx_1'=2,'gy_0'=4,'gy_1'=4] {'gx_0'}, use_global_device_ids=true, to_apply=%region_1.2 | all-reduce | flops 1 | bytes 8 | tf_op jit(solution)/shard_map/psum | solution.py:15
  157.2 11.1 %psum.254 = f32[]{:T(128)} all-reduce(f32[]{:T(128)} %psum.253), channel_id=1, replica_groups=mesh['gx_0'=4,'gx_1'=2,'gy_0'=4,'gy_1'=4] {'gy_0'}, use_global_device_ids=true, to_apply=%region_3.4 | all-reduce | flops 1 | bytes 8 | tf_op jit(solution)/shard_map/psum | solution.py:15
  168.3 9.3 %psum.255 = f32[]{:T(128)} all-reduce(f32[]{:T(128)} %psum.254), channel_id=1, replica_groups=mesh['gx_0'=4,'gx_1'=2,'gy_0'=4,'gy_1'=4] {'gy_1'}, use_global_device_ids=true, to_apply=%region_4.5 | all-reduce | flops 1 | bytes 8 | tf_op jit(solution)/shard_map/psum | solution.py:15
  191.5 12.6 %fusion.62 = f32[4,768,128]{1,2,0:T(8,128)S(1)} fusion(f32[4,768,768]{2,1,0:T(8,128)} %gather_fusion, f32[4,768,128]{1,2,0:T(8,128)S(1)} %broadcast_divide_fusion.3, f32[4,768,128]{1,2,0:T(8,128)S(1)} %copy-done.2), kind=kOutput, calls=%fused_computation.128 | convolution fusion | flops 3625058304 | bytes 14155776 | tf_op jit(solution)/shard_map/bpq,bqc->bpc/dot_general | solution.py:82
  204.1 6.6 %multiply_reduce_fusion.13 = (f32[]{:T(128)}, f32[4,768,128]{1,2,0:T(8,128)}) fusion(f32[4,768,128]{1,2,0:T(8,128)S(1)} %broadcast_divide_fusion.3, f32[4,768,128]{1,2,0:T(8,128)S(1)} %fusion.62, f32[4,128]{1,0:T(4,128)S(1)} %convert_multiply_fusion, f32[1,768,128]{1,2,0:T(8,128)S(1)} %collective-permute-done.4, ...), kind=kOutput, calls=%fused_computation.127 | convolution fusion | flops 3634495488 | bytes 7894020 | tf_op jit(solution)/shard_map/pq,xqy->xpy/dot_general | solution.py:75
  210.7 8.0 %psum.256 = f32[1]{0:T(128)} all-reduce(f32[1]{0:T(128)} %bitcast.5), channel_id=1, replica_groups=mesh['gx_0'=4,'gx_1'=2,'gy_0'=4,'gy_1'=4] {'gx_0'}, use_global_device_ids=true, to_apply=%region_6.7 | all-reduce | flops 1 | bytes 8 | tf_op jit(solution)/shard_map/psum | solution.py:15
  221.8 8.4 %psum.258 = f32[1]{0:T(128)} all-reduce(f32[1]{0:T(128)} %psum.257), channel_id=1, replica_groups=mesh['gx_0'=4,'gx_1'=2,'gy_0'=4,'gy_1'=4] {'gy_0'}, use_global_device_ids=true, to_apply=%region_8.9 | all-reduce | flops 1 | bytes 8 | tf_op jit(solution)/shard_map/psum | solution.py:15
  230.2 10.3 %psum.259 = f32[1]{0:T(128)} all-reduce(f32[1]{0:T(128)} %psum.258), channel_id=1, replica_groups=mesh['gx_0'=4,'gx_1'=2,'gy_0'=4,'gy_1'=4] {'gy_1'}, use_global_device_ids=true, to_apply=%region_9.10 | all-reduce | flops 1 | bytes 8 | tf_op jit(solution)/shard_map/psum | solution.py:15
  244.0 10.7 %psum.260 = f32[]{:T(128)} all-reduce(f32[]{:T(128)} %multiply_reduce_fusion.12), channel_id=1, replica_groups=mesh['gx_0'=4,'gx_1'=2,'gy_0'=4,'gy_1'=4] {'gx_0'}, use_global_device_ids=true, to_apply=%region_11.12 | all-reduce | flops 1 | bytes 8 | tf_op jit(solution)/shard_map/psum | solution.py:15
  257.9 9.8 %psum.262 = f32[]{:T(128)} all-reduce(f32[]{:T(128)} %psum.261), channel_id=1, replica_groups=mesh['gx_0'=4,'gx_1'=2,'gy_0'=4,'gy_1'=4] {'gy_0'}, use_global_device_ids=true, to_apply=%region_13.14 | all-reduce | flops 1 | bytes 8 | tf_op jit(solution)/shard_map/psum | solution.py:15
  267.7 11.0 %psum.263 = f32[]{:T(128)} all-reduce(f32[]{:T(128)} %psum.262), channel_id=1, replica_groups=mesh['gx_0'=4,'gx_1'=2,'gy_0'=4,'gy_1'=4] {'gy_1'}, use_global_device_ids=true, to_apply=%region_14.15 | all-reduce | flops 1 | bytes 8 | tf_op jit(solution)/shard_map/psum | solution.py:15
  284.3 3.9 collective-permute-start.11
  290.2 4.2 collective-permute-start.8
  294.4 12.6 %fusion.60 = f32[4,768,128]{1,2,0:T(8,128)S(1)} fusion(f32[4,768,768]{2,1,0:T(8,128)} %gather_fusion, f32[4,768,128]{1,2,0:T(8,128)S(1)} %broadcast_divide_fusion.2, f32[4,768,128]{1,2,0:T(8,128)S(1)} %copy-done.3), kind=kOutput, calls=%fused_computation.123 | convolution fusion | flops 3625058304 | bytes 14155776 | tf_op jit(solution)/shard_map/bpq,bqc->bpc/dot_general | solution.py:82
  307.0 6.7 %multiply_reduce_fusion.11 = (f32[]{:T(128)}, f32[]{:T(128)}, f32[4,768,128]{1,2,0:T(8,128)}) fusion(f32[4,768,128]{1,2,0:T(8,128)S(1)} %copy-done.10, f32[4,768,128]{1,2,0:T(8,128)S(1)} %broadcast_divide_fusion.2, f32[4,768,128]{1,2,0:T(8,128)S(1)} %fusion.60, f32[4,128]{1,0:T(4,128)S(1)} %convert_multiply_fusion, ...), kind=kOutput, calls=%fused_computation.122 | convolution fusion | flops 3635281920 | bytes 9466888 | tf_op jit(solution)/shard_map/pq,xqy->xpy/dot_general | solution.py:75
  315.0 6.5 %psum.264 = f32[2]{0:T(128)S(1)} all-reduce(f32[2]{0:T(128)S(1)} %pad_maximum_fusion.31), channel_id=1, replica_groups=mesh['gx_0'=4,'gx_1'=2,'gy_0'=4,'gy_1'=4] {'gx_0'}, use_global_device_ids=true, to_apply=%region_17.18 | all-reduce | flops 2 | bytes 16 | tf_op jit(solution)/shard_map/psum | solution.py:15
  324.0 7.7 %psum.266 = f32[2]{0:T(128)S(1)} all-reduce(f32[2]{0:T(128)S(1)} %psum.265), channel_id=1, replica_groups=mesh['gx_0'=4,'gx_1'=2,'gy_0'=4,'gy_1'=4] {'gy_0'}, use_global_device_ids=true, to_apply=%region_19.20 | all-reduce | flops 2 | bytes 16 | tf_op jit(solution)/shard_map/psum | solution.py:15
  331.7 9.2 %psum.267 = f32[2]{0:T(128)S(1)} all-reduce(f32[2]{0:T(128)S(1)} %psum.266), channel_id=1, replica_groups=mesh['gx_0'=4,'gx_1'=2,'gy_0'=4,'gy_1'=4] {'gy_1'}, use_global_device_ids=true, to_apply=%region_20.21 | all-reduce | flops 2 | bytes 16 | tf_op jit(solution)/shard_map/psum | solution.py:15
  341.5 5.7 multiply_reduce_fusion.9
  347.2 11.6 %psum.268 = f32[]{:T(128)} all-reduce(f32[]{:T(128)} %get-tuple-element.16), channel_id=1, replica_groups=mesh['gx_0'=4,'gx_1'=2,'gy_0'=4,'gy_1'=4] {'gx_0'}, use_global_device_ids=true, to_apply=%region_22.23 | all-reduce | flops 1 | bytes 8 | tf_op jit(solution)/shard_map/psum | solution.py:15
  362.0 9.9 %psum.270 = f32[]{:T(128)} all-reduce(f32[]{:T(128)} %psum.269), channel_id=1, replica_groups=mesh['gx_0'=4,'gx_1'=2,'gy_0'=4,'gy_1'=4] {'gy_0'}, use_global_device_ids=true, to_apply=%region_24.25 | all-reduce | flops 1 | bytes 8 | tf_op jit(solution)/shard_map/psum | solution.py:15
  371.9 11.6 %psum.271 = f32[]{:T(128)} all-reduce(f32[]{:T(128)} %psum.270), channel_id=1, replica_groups=mesh['gx_0'=4,'gx_1'=2,'gy_0'=4,'gy_1'=4] {'gy_1'}, use_global_device_ids=true, to_apply=%region_25.26 | all-reduce | flops 1 | bytes 8 | tf_op jit(solution)/shard_map/psum | solution.py:15
  388.0 3.9 collective-permute-start.15
  393.9 4.1 collective-permute-start.12
  398.0 12.6 %fusion.58 = f32[4,768,128]{1,2,0:T(8,128)S(1)} fusion(f32[4,768,768]{2,1,0:T(8,128)} %gather_fusion, f32[4,768,128]{1,2,0:T(8,128)S(1)} %broadcast_divide_fusion.1, f32[4,768,128]{1,2,0:T(8,128)S(1)} %copy-done.4), kind=kOutput, calls=%fused_computation.117 | convolution fusion | flops 3625058304 | bytes 14155776 | tf_op jit(solution)/shard_map/bpq,bqc->bpc/dot_general | solution.py:82
  410.6 6.9 %multiply_reduce_fusion.8 = (f32[]{:T(128)}, f32[]{:T(128)}, f32[]{:T(128)}, f32[4,768,128]{1,2,0:T(8,128)}) fusion(f32[4,768,128]{1,2,0:T(8,128)S(1)} %copy-done.11, f32[4,768,128]{1,2,0:T(8,128)S(1)} %broadcast_divide_fusion.1, f32[4,768,128]{1,2,0:T(8,128)S(1)} %copy-done.7, f32[4,768,128]{1,2,0:T(8,128)S(1)} %fusion.58, ...), kind=kOutput, calls=%fused_computation.116 | convolution fusion | flops 3636068352 | bytes 11039756 | tf_op jit(solution)/shard_map/pq,xqy->xpy/dot_general | solution.py:75
  419.5 6.5 %psum.272 = f32[3]{0:T(128)S(1)} all-reduce(f32[3]{0:T(128)S(1)} %pad_maximum_fusion.32), channel_id=1, replica_groups=mesh['gx_0'=4,'gx_1'=2,'gy_0'=4,'gy_1'=4] {'gx_0'}, use_global_device_ids=true, to_apply=%region_29.30 | all-reduce | flops 3 | bytes 24 | tf_op jit(solution)/shard_map/psum | solution.py:15
  428.4 7.7 %psum.274 = f32[3]{0:T(128)S(1)} all-reduce(f32[3]{0:T(128)S(1)} %psum.273), channel_id=1, replica_groups=mesh['gx_0'=4,'gx_1'=2,'gy_0'=4,'gy_1'=4] {'gy_0'}, use_global_device_ids=true, to_apply=%region_31.32 | all-reduce | flops 3 | bytes 24 | tf_op jit(solution)/shard_map/psum | solution.py:15
  436.2 9.2 %psum.275 = f32[3]{0:T(128)S(1)} all-reduce(f32[3]{0:T(128)S(1)} %psum.274), channel_id=1, replica_groups=mesh['gx_0'=4,'gx_1'=2,'gy_0'=4,'gy_1'=4] {'gy_1'}, use_global_device_ids=true, to_apply=%region_32.33 | all-reduce | flops 3 | bytes 24 | tf_op jit(solution)/shard_map/psum | solution.py:15
  446.0 7.1 %multiply_reduce_fusion.5 = (f32[]{:T(128)}, f32[4,768,128]{1,2,0:T(8,128)}) fusion(f32[]{:T(128)} %bitcast.22, f32[4,768,128]{1,2,0:T(8,128)} %copy-done.6, f32[]{:T(128)} %bitcast.21, f32[4,768,128]{1,2,0:T(8,128)} %get-tuple-element.66, f32[]{:T(128)} %bitcast.20, f32[4,768,128]{1,2,0:T(8,128)} %get-tuple-element.17, f32[]{:T(128)} %sqrt.17, ...), kind=kLoop, calls=%fused_computation.112 | loop fusion | flops 3932159 | bytes 7864344 | tf_op jit(solution)/shard_map/reduce_sum | solution.py:39
  453.0 11.6 %psum.276 = f32[]{:T(128)} all-reduce(f32[]{:T(128)} %get-tuple-element.14), channel_id=1, replica_groups=mesh['gx_0'=4,'gx_1'=2,'gy_0'=4,'gy_1'=4] {'gx_0'}, use_global_device_ids=true, to_apply=%region_34.35 | all-reduce | flops 1 | bytes 8 | tf_op jit(solution)/shard_map/psum | solution.py:15
  467.8 9.9 %psum.278 = f32[]{:T(128)} all-reduce(f32[]{:T(128)} %psum.277), channel_id=1, replica_groups=mesh['gx_0'=4,'gx_1'=2,'gy_0'=4,'gy_1'=4] {'gy_0'}, use_global_device_ids=true, to_apply=%region_36.37 | all-reduce | flops 1 | bytes 8 | tf_op jit(solution)/shard_map/psum | solution.py:15
  477.7 11.6 %psum.279 = f32[]{:T(128)} all-reduce(f32[]{:T(128)} %psum.278), channel_id=1, replica_groups=mesh['gx_0'=4,'gx_1'=2,'gy_0'=4,'gy_1'=4] {'gy_1'}, use_global_device_ids=true, to_apply=%region_37.38 | all-reduce | flops 1 | bytes 8 | tf_op jit(solution)/shard_map/psum | solution.py:15
  499.6 4.1 collective-permute-start.16
  503.7 12.6 %fusion.56 = f32[4,768,128]{1,2,0:T(8,128)S(1)} fusion(f32[4,768,768]{2,1,0:T(8,128)} %gather_fusion, f32[4,768,128]{1,2,0:T(8,128)S(1)} %broadcast_divide_fusion, f32[4,768,128]{1,2,0:T(8,128)S(1)} %copy-done.5), kind=kOutput, calls=%fused_computation.110 | convolution fusion | flops 3625058304 | bytes 14155776 | tf_op jit(solution)/shard_map/bpq,bqc->bpc/dot_general | solution.py:82
  516.4 7.0 %multiply_reduce_fusion.4 = (f32[]{:T(128)}, f32[]{:T(128)}, f32[]{:T(128)}, f32[]{:T(128)}, f32[4,768,128]{1,2,0:T(8,128)}) fusion(f32[4,768,128]{1,2,0:T(8,128)S(1)} %copy-done.12, f32[4,768,128]{1,2,0:T(8,128)S(1)} %broadcast_divide_fusion, f32[4,768,128]{1,2,0:T(8,128)S(1)} %copy-done.14, f32[4,768,128]{1,2,0:T(8,128)S(1)} %copy-done.8, ...), kind=kOutput, calls=%fused_computation.109 | convolution fusion | flops 3636854784 | bytes 12612624 | tf_op jit(solution)/shard_map/pq,xqy->xpy/dot_general | solution.py:75
  526.0 6.5 %psum.280 = f32[4]{0:T(128)S(1)} all-reduce(f32[4]{0:T(128)S(1)} %pad_maximum_fusion.33), channel_id=1, replica_groups=mesh['gx_0'=4,'gx_1'=2,'gy_0'=4,'gy_1'=4] {'gx_0'}, use_global_device_ids=true, to_apply=%region_42.43 | all-reduce | flops 4 | bytes 32 | tf_op jit(solution)/shard_map/psum | solution.py:15
  535.0 7.7 %psum.282 = f32[4]{0:T(128)S(1)} all-reduce(f32[4]{0:T(128)S(1)} %psum.281), channel_id=1, replica_groups=mesh['gx_0'=4,'gx_1'=2,'gy_0'=4,'gy_1'=4] {'gy_0'}, use_global_device_ids=true, to_apply=%region_44.45 | all-reduce | flops 4 | bytes 32 | tf_op jit(solution)/shard_map/psum | solution.py:15
  542.7 9.2 %psum.283 = f32[4]{0:T(128)S(1)} all-reduce(f32[4]{0:T(128)S(1)} %psum.282), channel_id=1, replica_groups=mesh['gx_0'=4,'gx_1'=2,'gy_0'=4,'gy_1'=4] {'gy_1'}, use_global_device_ids=true, to_apply=%region_45.46 | all-reduce | flops 4 | bytes 32 | tf_op jit(solution)/shard_map/psum | solution.py:15
  552.6 7.1 %multiply_reduce_fusion = f32[]{:T(128)} fusion(f32[4,768,128]{1,2,0:T(8,128)} %copy-done.6, f32[4,768,128]{1,2,0:T(8,128)} %get-tuple-element.67, f32[]{:T(128)} %bitcast.33, f32[]{:T(128)} %bitcast.32, f32[]{:T(128)} %bitcast.31, f32[]{:T(128)} %bitcast.30, f32[4,768,128]{1,2,0:T(8,128)} %get-tuple-element.15, f32[]{:T(128)} %sqrt.18, ...), kind=kLoop, calls=%fused_computation.105 | loop fusion | flops 5111807 | bytes 7864352 | tf_op jit(solution)/shard_map/reduce_sum | solution.py:39
  559.7 11.6 %psum.284 = f32[]{:T(128)} all-reduce(f32[]{:T(128)} %multiply_reduce_fusion), channel_id=1, replica_groups=mesh['gx_0'=4,'gx_1'=2,'gy_0'=4,'gy_1'=4] {'gx_0'}, use_global_device_ids=true, to_apply=%region_47.48 | all-reduce | flops 1 | bytes 8 | tf_op jit(solution)/shard_map/psum | solution.py:15
  575.1 9.8 %psum.286 = f32[]{:T(128)} all-reduce(f32[]{:T(128)} %psum.285), channel_id=1, replica_groups=mesh['gx_0'=4,'gx_1'=2,'gy_0'=4,'gy_1'=4] {'gy_0'}, use_global_device_ids=true, to_apply=%region_49.50 | all-reduce | flops 1 | bytes 8 | tf_op jit(solution)/shard_map/psum | solution.py:15
  585.0 11.6 %psum.287 = f32[]{:T(128)} all-reduce(f32[]{:T(128)} %psum.286), channel_id=1, replica_groups=mesh['gx_0'=4,'gx_1'=2,'gy_0'=4,'gy_1'=4] {'gy_1'}, use_global_device_ids=true, to_apply=%region_50.51 | all-reduce | flops 1 | bytes 8 | tf_op jit(solution)/shard_map/psum | solution.py:15
  616.1 5.0 multiply_add_fusion
  (130 shorter events, 100.8 us)
Async XLA Ops:
  6.5 127.1 %copy-start = (f32[768,768]{1,0:T(8,128)S(1)}, f32[768,768]{1,0:T(8,128)}, u32[]{:S(2)}) copy-start(f32[768,768]{1,0:T(8,128)} %param.9) | copy-start | bytes 7077892
  6.5 102.1 %all-gather.2.cloned.1.call-start = ((), (), s32[]{:S(2)}) async-start(), calls=%async_computation | async-start | bytes 21233664 | tf_op jit(solution)/shard_map/all_gather | solution.py:78
  11.3 122.3 %collective-permute-start.2 = (f32[4,768,1]{1,2,0:T(1,128)S(1)}, f32[4,768,1]{1,2,0:T(1,128)S(1)}, u32[]{:S(2)}, u32[]{:S(2)}) collective-permute-start(f32[4,768,1]{1,2,0:T(1,128)S(1)} %get-tuple-element.34), channel_id=1, source_target_pairs={{1,0},{2,1},{3,2},{4,3},{5,4},{6,5},{7,6},{8,7},{9,8},{10,9},{11,1... | collective-permute-start | bytes 36872 | tf_op jit(solution)/shard_map/ppermute | solution.py:27
  13.3 120.3 %collective-permute-start.3 = (f32[4,768,1]{1,2,0:T(1,128)S(1)}, f32[4,768,1]{1,2,0:T(1,128)S(1)}, u32[]{:S(2)}, u32[]{:S(2)}) collective-permute-start(f32[4,768,1]{1,2,0:T(1,128)S(1)} %get-tuple-element.35), channel_id=1, source_target_pairs={{0,1},{1,2},{2,3},{3,4},{4,5},{5,6},{6,7},{7,8},{8,9},{9,10},{10,1... | collective-permute-start | bytes 36872 | tf_op jit(solution)/shard_map/ppermute | solution.py:26
  18.3 115.3 %collective-permute-start.1 = (f32[1,768,128]{1,2,0:T(8,128)S(1)}, f32[1,768,128]{1,2,0:T(8,128)}, u32[]{:S(2)}, u32[]{:S(2)}) collective-permute-start(f32[1,768,128]{1,2,0:T(8,128)S(1)} %get-tuple-element.36), channel_id=1, source_target_pairs={{0,16},{16,32},{32,48},{48,64},{64,80},{80,96},{96,112},{1,17},{17... | collective-permute-start | bytes 1179656 | tf_op jit(solution)/shard_map/ppermute | solution.py:26
  20.2 7.1 %copy-start.19 = (s32[1,4,1]{1,2,0:T(1,128)S(1)}, s32[1,4,1]{1,2,0:T(1,128)}, u32[]{:S(2)}) copy-start(s32[1,4,1]{1,2,0:T(1,128)} %param.12) | copy-start | bytes 52
  20.3 7.1 %copy-start.17 = (s32[4,128]{1,0:T(4,128)S(1)}, s32[4,128]{1,0:T(4,128)}, u32[]{:S(2)}) copy-start(s32[4,128]{1,0:T(4,128)} %param.11) | copy-start | bytes 6148
  20.3 113.3 %collective-permute-start = (f32[1,768,128]{1,2,0:T(8,128)S(1)}, f32[1,768,128]{1,2,0:T(8,128)}, u32[]{:S(2)}, u32[]{:S(2)}) collective-permute-start(f32[1,768,128]{1,2,0:T(8,128)S(1)} %get-tuple-element.37), channel_id=1, source_target_pairs={{16,0},{32,16},{48,32},{64,48},{80,64},{96,80},{112,96},{17,1},{33... | collective-permute-start | bytes 1179656 | tf_op jit(solution)/shard_map/ppermute | solution.py:27
  119.9 13.7 %copy-start.1 = (f32[4,768,128]{1,2,0:T(8,128)S(1)}, f32[4,768,128]{1,2,0:T(8,128)}, u32[]{:S(2)}) copy-start(f32[4,768,128]{1,2,0:T(8,128)} %copy.40) | copy-start | bytes 4718596
  119.9 13.7 %copy-start.15 = (f32[4,768,128]{2,1,0:T(8,128)S(1)}, f32[4,768,128]{2,1,0:T(8,128)}, u32[]{:S(2)}) copy-start(f32[4,768,128]{2,1,0:T(8,128)} %param.7) | copy-start | bytes 4718596
  119.9 13.7 %copy-start.16 = (f32[4,768,128]{1,2,0:T(8,128)S(1)}, f32[4,768,128]{1,2,0:T(8,128)}, u32[]{:S(2)}) copy-start(f32[4,768,128]{1,2,0:T(8,128)} %copy.36) | copy-start | bytes 4718596
  119.9 13.7 %copy-start.18 = (f32[768]{0:T(1024)S(1)}, f32[768]{0:T(1024)}, u32[]{:S(2)}) copy-start(f32[768]{0:T(1024)} %param.10) | copy-start | bytes 9220
  179.7 24.4 %copy-start.9 = (f32[4,768,128]{1,2,0:T(8,128)}, f32[4,768,128]{1,2,0:T(8,128)S(1)}, u32[]{:S(2)}) copy-start(f32[4,768,128]{1,2,0:T(8,128)S(1)} %broadcast_divide_fusion.3) | copy-start | bytes 4718596
  179.7 11.8 %copy-start.2 = (f32[4,768,128]{1,2,0:T(8,128)S(1)}, f32[4,768,128]{1,2,0:T(8,128)}, u32[]{:S(2)}) copy-start(f32[4,768,128]{1,2,0:T(8,128)} %copy.40) | copy-start | bytes 4718596
  179.8 24.3 %collective-permute-start.6 = (f32[4,768,1]{1,2,0:T(1,128)S(1)}, f32[4,768,1]{1,2,0:T(1,128)S(1)}, u32[]{:S(2)}, u32[]{:S(2)}) collective-permute-start(f32[4,768,1]{1,2,0:T(1,128)S(1)} %get-tuple-element.30), channel_id=1, source_target_pairs={{1,0},{2,1},{3,2},{4,3},{5,4},{6,5},{7,6},{8,7},{9,8},{10,9},{11,1... | collective-permute-start | bytes 36872 | tf_op jit(solution)/shard_map/ppermute | solution.py:27
  183.5 20.6 %collective-permute-start.7 = (f32[4,768,1]{1,2,0:T(1,128)S(1)}, f32[4,768,1]{1,2,0:T(1,128)S(1)}, u32[]{:S(2)}, u32[]{:S(2)}) collective-permute-start(f32[4,768,1]{1,2,0:T(1,128)S(1)} %get-tuple-element.31), channel_id=1, source_target_pairs={{0,1},{1,2},{2,3},{3,4},{4,5},{5,6},{6,7},{7,8},{8,9},{9,10},{10,1... | collective-permute-start | bytes 36872 | tf_op jit(solution)/shard_map/ppermute | solution.py:26
  185.9 18.2 %collective-permute-start.5 = (f32[1,768,128]{1,2,0:T(8,128)S(1)}, f32[1,768,128]{1,2,0:T(8,128)S(1)}, u32[]{:S(2)}, u32[]{:S(2)}) collective-permute-start(f32[1,768,128]{1,2,0:T(8,128)S(1)} %get-tuple-element.32), channel_id=1, source_target_pairs={{0,16},{16,32},{32,48},{48,64},{64,80},{80,96},{96,112},{1,17},{17... | collective-permute-start | bytes 1179656 | tf_op jit(solution)/shard_map/ppermute | solution.py:26
  187.8 16.3 %collective-permute-start.4 = (f32[1,768,128]{1,2,0:T(8,128)S(1)}, f32[1,768,128]{1,2,0:T(8,128)S(1)}, u32[]{:S(2)}, u32[]{:S(2)}) collective-permute-start(f32[1,768,128]{1,2,0:T(8,128)S(1)} %get-tuple-element.33), channel_id=1, source_target_pairs={{16,0},{32,16},{48,32},{64,48},{80,64},{96,80},{112,96},{17,1},{33... | collective-permute-start | bytes 1179656 | tf_op jit(solution)/shard_map/ppermute | solution.py:27
  282.0 25.0 %copy-start.6 = (f32[4,768,128]{1,2,0:T(8,128)}, f32[4,768,128]{1,2,0:T(8,128)S(1)}, u32[]{:S(2)}) copy-start(f32[4,768,128]{1,2,0:T(8,128)S(1)} %broadcast_divide_fusion.2) | copy-start | bytes 4718596
  282.0 12.3 %copy-start.3 = (f32[4,768,128]{1,2,0:T(8,128)S(1)}, f32[4,768,128]{1,2,0:T(8,128)}, u32[]{:S(2)}) copy-start(f32[4,768,128]{1,2,0:T(8,128)} %copy.40) | copy-start | bytes 4718596
  282.1 24.8 %collective-permute-start.10 = (f32[4,768,1]{1,2,0:T(1,128)S(1)}, f32[4,768,1]{1,2,0:T(1,128)S(1)}, u32[]{:S(2)}, u32[]{:S(2)}) collective-permute-start(f32[4,768,1]{1,2,0:T(1,128)S(1)} %get-tuple-element.26), channel_id=1, source_target_pairs={{1,0},{2,1},{3,2},{4,3},{5,4},{6,5},{7,6},{8,7},{9,8},{10,9},{11,1... | collective-permute-start | bytes 36872 | tf_op jit(solution)/shard_map/ppermute | solution.py:27
  284.3 22.6 %collective-permute-start.11 = (f32[4,768,1]{1,2,0:T(1,128)S(1)}, f32[4,768,1]{1,2,0:T(1,128)S(1)}, u32[]{:S(2)}, u32[]{:S(2)}) collective-permute-start(f32[4,768,1]{1,2,0:T(1,128)S(1)} %get-tuple-element.27), channel_id=1, source_target_pairs={{0,1},{1,2},{2,3},{3,4},{4,5},{5,6},{6,7},{7,8},{8,9},{9,10},{10,1... | collective-permute-start | bytes 36872 | tf_op jit(solution)/shard_map/ppermute | solution.py:26
  288.2 18.7 %collective-permute-start.9 = (f32[1,768,128]{1,2,0:T(8,128)S(1)}, f32[1,768,128]{1,2,0:T(8,128)S(1)}, u32[]{:S(2)}, u32[]{:S(2)}) collective-permute-start(f32[1,768,128]{1,2,0:T(8,128)S(1)} %get-tuple-element.28), channel_id=1, source_target_pairs={{0,16},{16,32},{32,48},{48,64},{64,80},{80,96},{96,112},{1,17},{17... | collective-permute-start | bytes 1179656 | tf_op jit(solution)/shard_map/ppermute | solution.py:26
  290.2 16.8 %copy-start.10 = (f32[4,768,128]{1,2,0:T(8,128)S(1)}, f32[4,768,128]{1,2,0:T(8,128)}, u32[]{:S(2)}) copy-start(f32[4,768,128]{1,2,0:T(8,128)} %copy-done.9) | copy-start | bytes 4718596
  290.2 16.8 %collective-permute-start.8 = (f32[1,768,128]{1,2,0:T(8,128)S(1)}, f32[1,768,128]{1,2,0:T(8,128)S(1)}, u32[]{:S(2)}, u32[]{:S(2)}) collective-permute-start(f32[1,768,128]{1,2,0:T(8,128)S(1)} %get-tuple-element.29), channel_id=1, source_target_pairs={{16,0},{32,16},{48,32},{64,48},{80,64},{96,80},{112,96},{17,1},{33... | collective-permute-start | bytes 1179656 | tf_op jit(solution)/shard_map/ppermute | solution.py:27
  385.7 24.9 %copy-start.13 = (f32[4,768,128]{1,2,0:T(8,128)}, f32[4,768,128]{1,2,0:T(8,128)S(1)}, u32[]{:S(2)}) copy-start(f32[4,768,128]{1,2,0:T(8,128)S(1)} %broadcast_divide_fusion.1) | copy-start | bytes 4718596
  385.7 12.3 %copy-start.4 = (f32[4,768,128]{1,2,0:T(8,128)S(1)}, f32[4,768,128]{1,2,0:T(8,128)}, u32[]{:S(2)}) copy-start(f32[4,768,128]{1,2,0:T(8,128)} %copy.40) | copy-start | bytes 4718596
  385.8 24.7 %collective-permute-start.14 = (f32[4,768,1]{1,2,0:T(1,128)S(1)}, f32[4,768,1]{1,2,0:T(1,128)S(1)}, u32[]{:S(2)}, u32[]{:S(2)}) collective-permute-start(f32[4,768,1]{1,2,0:T(1,128)S(1)} %get-tuple-element.22), channel_id=1, source_target_pairs={{1,0},{2,1},{3,2},{4,3},{5,4},{6,5},{7,6},{8,7},{9,8},{10,9},{11,1... | collective-permute-start | bytes 36872 | tf_op jit(solution)/shard_map/ppermute | solution.py:27
  388.0 22.5 %collective-permute-start.15 = (f32[4,768,1]{1,2,0:T(1,128)S(1)}, f32[4,768,1]{1,2,0:T(1,128)S(1)}, u32[]{:S(2)}, u32[]{:S(2)}) collective-permute-start(f32[4,768,1]{1,2,0:T(1,128)S(1)} %get-tuple-element.23), channel_id=1, source_target_pairs={{0,1},{1,2},{2,3},{3,4},{4,5},{5,6},{6,7},{7,8},{8,9},{9,10},{10,1... | collective-permute-start | bytes 36872 | tf_op jit(solution)/shard_map/ppermute | solution.py:26
  391.9 18.6 %collective-permute-start.13 = (f32[1,768,128]{1,2,0:T(8,128)S(1)}, f32[1,768,128]{1,2,0:T(8,128)S(1)}, u32[]{:S(2)}, u32[]{:S(2)}) collective-permute-start(f32[1,768,128]{1,2,0:T(8,128)S(1)} %get-tuple-element.24), channel_id=1, source_target_pairs={{0,16},{16,32},{32,48},{48,64},{64,80},{80,96},{96,112},{1,17},{17... | collective-permute-start | bytes 1179656 | tf_op jit(solution)/shard_map/ppermute | solution.py:26
  393.9 16.7 %copy-start.7 = (f32[4,768,128]{1,2,0:T(8,128)S(1)}, f32[4,768,128]{1,2,0:T(8,128)}, u32[]{:S(2)}) copy-start(f32[4,768,128]{1,2,0:T(8,128)} %copy-done.6) | copy-start | bytes 4718596
  393.9 16.7 %copy-start.11 = (f32[4,768,128]{1,2,0:T(8,128)S(1)}, f32[4,768,128]{1,2,0:T(8,128)}, u32[]{:S(2)}) copy-start(f32[4,768,128]{1,2,0:T(8,128)} %copy-done.9) | copy-start | bytes 4718596
  393.9 16.7 %collective-permute-start.12 = (f32[1,768,128]{1,2,0:T(8,128)S(1)}, f32[1,768,128]{1,2,0:T(8,128)S(1)}, u32[]{:S(2)}, u32[]{:S(2)}) collective-permute-start(f32[1,768,128]{1,2,0:T(8,128)S(1)} %get-tuple-element.25), channel_id=1, source_target_pairs={{16,0},{32,16},{48,32},{64,48},{80,64},{96,80},{112,96},{17,1},{33... | collective-permute-start | bytes 1179656 | tf_op jit(solution)/shard_map/ppermute | solution.py:27
  491.6 12.2 %copy-start.5 = (f32[4,768,128]{1,2,0:T(8,128)S(1)}, f32[4,768,128]{1,2,0:T(8,128)}, u32[]{:S(2)}) copy-start(f32[4,768,128]{1,2,0:T(8,128)} %copy.40) | copy-start | bytes 4718596
  491.7 24.7 %collective-permute-start.18 = (f32[4,768,1]{1,2,0:T(1,128)S(1)}, f32[4,768,1]{1,2,0:T(1,128)S(1)}, u32[]{:S(2)}, u32[]{:S(2)}) collective-permute-start(f32[4,768,1]{1,2,0:T(1,128)S(1)} %get-tuple-element.18), channel_id=1, source_target_pairs={{1,0},{2,1},{3,2},{4,3},{5,4},{6,5},{7,6},{8,7},{9,8},{10,9},{11,1... | collective-permute-start | bytes 36872 | tf_op jit(solution)/shard_map/ppermute | solution.py:27
  493.7 22.6 %collective-permute-start.19 = (f32[4,768,1]{1,2,0:T(1,128)S(1)}, f32[4,768,1]{1,2,0:T(1,128)S(1)}, u32[]{:S(2)}, u32[]{:S(2)}) collective-permute-start(f32[4,768,1]{1,2,0:T(1,128)S(1)} %get-tuple-element.19), channel_id=1, source_target_pairs={{0,1},{1,2},{2,3},{3,4},{4,5},{5,6},{6,7},{7,8},{8,9},{9,10},{10,1... | collective-permute-start | bytes 36872 | tf_op jit(solution)/shard_map/ppermute | solution.py:26
  497.7 18.7 %collective-permute-start.17 = (f32[1,768,128]{1,2,0:T(8,128)S(1)}, f32[1,768,128]{1,2,0:T(8,128)S(1)}, u32[]{:S(2)}, u32[]{:S(2)}) collective-permute-start(f32[1,768,128]{1,2,0:T(8,128)S(1)} %get-tuple-element.20), channel_id=1, source_target_pairs={{0,16},{16,32},{32,48},{48,64},{64,80},{80,96},{96,112},{1,17},{17... | collective-permute-start | bytes 1179656 | tf_op jit(solution)/shard_map/ppermute | solution.py:26
  499.6 16.8 %copy-start.8 = (f32[4,768,128]{1,2,0:T(8,128)S(1)}, f32[4,768,128]{1,2,0:T(8,128)}, u32[]{:S(2)}) copy-start(f32[4,768,128]{1,2,0:T(8,128)} %copy-done.6) | copy-start | bytes 4718596
  499.6 16.8 %copy-start.12 = (f32[4,768,128]{1,2,0:T(8,128)S(1)}, f32[4,768,128]{1,2,0:T(8,128)}, u32[]{:S(2)}) copy-start(f32[4,768,128]{1,2,0:T(8,128)} %copy-done.9) | copy-start | bytes 4718596
  499.6 16.8 %copy-start.14 = (f32[4,768,128]{1,2,0:T(8,128)S(1)}, f32[4,768,128]{1,2,0:T(8,128)}, u32[]{:S(2)}) copy-start(f32[4,768,128]{1,2,0:T(8,128)} %copy-done.13) | copy-start | bytes 4718596
  499.6 16.7 %collective-permute-start.16 = (f32[1,768,128]{1,2,0:T(8,128)S(1)}, f32[1,768,128]{1,2,0:T(8,128)S(1)}, u32[]{:S(2)}, u32[]{:S(2)}) collective-permute-start(f32[1,768,128]{1,2,0:T(8,128)S(1)} %get-tuple-element.21), channel_id=1, source_target_pairs={{16,0},{32,16},{48,32},{64,48},{80,64},{96,80},{112,96},{17,1},{33... | collective-permute-start | bytes 1179656 | tf_op jit(solution)/shard_map/ppermute | solution.py:27
Sparse Core Ops, SparseCore 0:
  9.0 99.6 all-gather.1
where the time goes:
time: 643 us; the launch traced here: 631 us
  blocking collectives  283 us (44%)
  matrix products  103 us (16%)
  waiting for transfers between devices  82.1 us (13%)
  starting transfers between devices  59.5 us (9%)
  other arithmetic  44.2 us (7%)
  between operations  33.5 us (5%)
  local copies, waits for them, and re-layouts  26.4 us (4%)
    psum x36, blocking collectives, one_axis_at_a_time(): return functools.reduce(lax.psum, axes, array)  283 us
    all_gather x1, waiting for transfers between devices, local(): every_op = lax.all_gather(correction_ops, GX, axis=0, tiled=True)  81.3 us
    dot_general x5, matrix products, correct(): jnp.einsum('bpq,bqc->bpc', chosen, field, precision=highest) * weights  63.9 us
    dot_general x5, matrix products, spread(): mixed = jnp.einsum('pq,xqy->xpy', vertical_mix, field, precision=highest)  38.6 us
    ppermute x10, starting transfers between devices, padded_2(): lax.ppermute(first, axis, [(b, a) for a, b in up])  31.9 us
    ppermute x10, starting transfers between devices, padded_2(): lax.ppermute(last, axis, up)  27.6 us
    reduce_sum x4, other arithmetic, squares(): return one_axis_at_a_time(jnp.sum(field * field), GX_GY)  23.4 us
  transfers between devices with their start and end apart: 21, of which 1 were waited for; matrix products, arithmetic and copies ran while one was open for 13% of the time, Pallas kernels for 0%

commit v1 on v0

--- a/solution.py
+++ b/solution.py
@@ -75,7 +75,9 @@
         mixed = jnp.einsum("pq,xqy->xpy", vertical_mix, field, precision=highest)
         return 2.0 * field + mixed + coeff_rows * lap
 
-    every_op = lax.all_gather(correction_ops, GX, axis=0, tiled=True)
+    every_op = jnp.concatenate(
+        lax.all_to_all(jnp.stack([correction_ops] * lax.psum(1, GX)), GX, 0, 0), 0
+    )
     chosen = every_op[regimes]
 
     def correct(field):

time: 643 us -> 739 us (1.15); the launches traced: 631 us -> 735 us
  waiting for transfers between devices: 82.1 us -> 187 us
  between operations: 33.5 us -> 19.6 us
  local copies, waits for them, and re-layouts: 26.4 us -> 35.9 us
    all_to_all x0 -> x1, waiting for transfers between devices: none -> 187 us  [local(): lax.all_to_all(jnp.stack([correction_ops] * lax.psum(1, GX)), GX, 0, 0)]
    all_gather x1 -> x0, waiting for transfers between devices: 81.3 us -> none  [local(): every_op = lax.all_gather(correction_ops, GX, axis=0, tiled=True)]
    another operation x2 -> x3, local copies, waits for them, and re-layouts: 0.01 us -> 9.89 us  [the longest x1 9.89 us: local(): jnp.stack([correction_ops] * lax.psum(1, GX))]
    ppermute x10, starting transfers between devices: 31.9 us -> 23.2 us  [padded_2(): lax.ppermute(first, axis, [(b, a) for a, b in up])]
  transfers between devices with their start and end apart: 21 -> 21, of which waited for: 1 -> 1; matrix products, arithmetic and copies ran while one was open for 13% -> 11% of each run, Pallas kernels for 0% -> 0%
where the time goes in v1:
time: 739 us; the launch traced here: 735 us
  blocking collectives  285 us (39%)
  waiting for transfers between devices  187 us (25%)
  matrix products  103 us (14%)
  starting transfers between devices  60.4 us (8%)
  other arithmetic  44.1 us (6%)
  local copies, waits for them, and re-layouts  35.9 us (5%)
  between operations  19.6 us (3%)
    psum x36, blocking collectives, one_axis_at_a_time(): return functools.reduce(lax.psum, axes, array)  285 us
    all_to_all x1, waiting for transfers between devices, local(): lax.all_to_all(jnp.stack([correction_ops] * lax.psum(1, GX)), GX, 0, 0)  187 us
    dot_general x5, matrix products, correct(): jnp.einsum('bpq,bqc->bpc', chosen, field, precision=highest) * weights  63.9 us
    dot_general x5, matrix products, spread(): mixed = jnp.einsum('pq,xqy->xpy', vertical_mix, field, precision=highest)  38.6 us
    ppermute x10, starting transfers between devices, padded_2(): lax.ppermute(last, axis, up)  30.9 us
    reduce_sum x4, other arithmetic, squares(): return one_axis_at_a_time(jnp.sum(field * field), GX_GY)  23.3 us
    ppermute x10, starting transfers between devices, padded_2(): lax.ppermute(first, axis, [(b, a) for a, b in up])  23.2 us
  transfers between devices with their start and end apart: 21, of which 1 were waited for; matrix products, arithmetic and copies ran while one was open for 11% of the time, Pallas kernels for 0%

profile of v1, /device:TPU:34, one launch (start us, length us, event | category | flops | bytes accessed | tf_op | source)
XLA Modules:
  0.0 734.8 jit_solution(16471709997994042430)
XLA Ops:
  0.0 9.9 %stack.65 = f32[8,1,768,768]{3,2,1,0:T(8,128)} broadcast(f32[768,768]{1,0:T(8,128)} %bitcast.117), dimensions={2,3} | broadcast | bytes 21233664 | tf_op jit(solution)/shard_map/stack | solution.py:79
  9.9 6.3 all-to-all-start
  34.9 187.1 %all-to-all-done = f32[8,1,768,768]{3,2,1,0:T(8,128)} async-done(((f32[8,1,768,768]{3,2,1,0:T(8,128)}), f32[8,1,768,768]{3,2,1,0:T(8,128)}, u32[]{:S(2)}, u32[]{:S(2)}) %all-to-all-start) | async-done | bytes 18874400 | tf_op jit(solution)/shard_map/all_to_all | solution.py:79
  221.9 11.2 %gather_fusion = f32[4,768,768]{2,1,0:T(8,128)} fusion(f32[8,768,768]{2,1,0:T(8,128)} %bitcast.3, s32[1024]{0:T(1024)S(1)} %pad_clamp_fusion), kind=kCustom, calls=%fused_computation | custom fusion | bytes 18874384 | tf_op jit(solution)/shard_map/gather | solution.py:81
  233.2 13.7 %fusion.74 = f32[4,768,128]{1,2,0:T(8,128)S(1)} fusion(f32[4,768,768]{2,1,0:T(8,128)} %gather_fusion, f32[4,768,128]{1,2,0:T(8,128)} %copy.23), kind=kOutput, calls=%fused_computation.132 | convolution fusion | flops 3623878656 | bytes 12582912 | tf_op jit(solution)/shard_map/bpq,bqc->bpc/dot_general | solution.py:84
  247.0 11.3 %multiply_reduce_fusion.14 = (f32[]{:T(128)}, f32[4,768,128]{1,2,0:T(8,128)}) fusion(f32[4,768,128]{1,2,0:T(8,128)S(1)} %copy-done.16, f32[4,768,128]{1,2,0:T(8,128)S(1)} %fusion.74, f32[4,128]{1,0:T(4,128)S(1)} %convert_multiply_fusion, f32[1,768,128]{1,2,0:T(8,128)} %collective-permute-done, f32[4,768,128]{1,2,0:T(8,128)S(1)} %copy-done.1, ...), kind=kOutput, calls=%fused_computation.131 | convolution fusion | flops 3634888704 | bytes 11039748 | tf_op jit(solution)/shard_map/pq,xqy->xpy/dot_general | solution.py:75
  258.3 10.3 %psum.252 = f32[]{:T(128)} all-reduce(f32[]{:T(128)} %get-tuple-element.61), channel_id=1, replica_groups=mesh['gx_0'=4,'gx_1'=2,'gy_0'=4,'gy_1'=4] {'gx_0'}, use_global_device_ids=true, to_apply=%region_1.2 | all-reduce | flops 1 | bytes 8 | tf_op jit(solution)/shard_map/psum | solution.py:15
  271.7 11.6 %psum.254 = f32[]{:T(128)} all-reduce(f32[]{:T(128)} %psum.253), channel_id=1, replica_groups=mesh['gx_0'=4,'gx_1'=2,'gy_0'=4,'gy_1'=4] {'gy_0'}, use_global_device_ids=true, to_apply=%region_3.4 | all-reduce | flops 1 | bytes 8 | tf_op jit(solution)/shard_map/psum | solution.py:15
  283.3 9.7 %psum.255 = f32[]{:T(128)} all-reduce(f32[]{:T(128)} %psum.254), channel_id=1, replica_groups=mesh['gx_0'=4,'gx_1'=2,'gy_0'=4,'gy_1'=4] {'gy_1'}, use_global_device_ids=true, to_apply=%region_4.5 | all-reduce | flops 1 | bytes 8 | tf_op jit(solution)/shard_map/psum | solution.py:15
  299.9 4.7 collective-permute-start.6
  306.6 12.6 %fusion.62 = f32[4,768,128]{1,2,0:T(8,128)S(1)} fusion(f32[4,768,768]{2,1,0:T(8,128)} %gather_fusion, f32[4,768,128]{1,2,0:T(8,128)S(1)} %broadcast_divide_fusion.3, f32[4,768,128]{1,2,0:T(8,128)S(1)} %copy-done.2), kind=kOutput, calls=%fused_computation.128 | convolution fusion | flops 3625058304 | bytes 14155776 | tf_op jit(solution)/shard_map/bpq,bqc->bpc/dot_general | solution.py:84
  319.2 6.6 multiply_reduce_fusion.13
  325.8 8.9 %psum.256 = f32[1]{0:T(128)} all-reduce(f32[1]{0:T(128)} %bitcast.7), channel_id=1, replica_groups=mesh['gx_0'=4,'gx_1'=2,'gy_0'=4,'gy_1'=4] {'gx_0'}, use_global_device_ids=true, to_apply=%region_6.7 | all-reduce | flops 1 | bytes 8 | tf_op jit(solution)/shard_map/psum | solution.py:15
  337.8 8.3 %psum.258 = f32[1]{0:T(128)} all-reduce(f32[1]{0:T(128)} %psum.257), channel_id=1, replica_groups=mesh['gx_0'=4,'gx_1'=2,'gy_0'=4,'gy_1'=4] {'gy_0'}, use_global_device_ids=true, to_apply=%region_8.9 | all-reduce | flops 1 | bytes 8 | tf_op jit(solution)/shard_map/psum | solution.py:15
  346.2 10.3 %psum.259 = f32[1]{0:T(128)} all-reduce(f32[1]{0:T(128)} %psum.258), channel_id=1, replica_groups=mesh['gx_0'=4,'gx_1'=2,'gy_0'=4,'gy_1'=4] {'gy_1'}, use_global_device_ids=true, to_apply=%region_9.10 | all-reduce | flops 1 | bytes 8 | tf_op jit(solution)/shard_map/psum | solution.py:15
  360.0 9.9 %psum.260 = f32[]{:T(128)} all-reduce(f32[]{:T(128)} %multiply_reduce_fusion.12), channel_id=1, replica_groups=mesh['gx_0'=4,'gx_1'=2,'gy_0'=4,'gy_1'=4] {'gx_0'}, use_global_device_ids=true, to_apply=%region_11.12 | all-reduce | flops 1 | bytes 8 | tf_op jit(solution)/shard_map/psum | solution.py:15
  373.0 10.4 %psum.262 = f32[]{:T(128)} all-reduce(f32[]{:T(128)} %psum.261), channel_id=1, replica_groups=mesh['gx_0'=4,'gx_1'=2,'gy_0'=4,'gy_1'=4] {'gy_0'}, use_global_device_ids=true, to_apply=%region_13.14 | all-reduce | flops 1 | bytes 8 | tf_op jit(solution)/shard_map/psum | solution.py:15
  383.5 10.3 %psum.263 = f32[]{:T(128)} all-reduce(f32[]{:T(128)} %psum.262), channel_id=1, replica_groups=mesh['gx_0'=4,'gx_1'=2,'gy_0'=4,'gy_1'=4] {'gy_1'}, use_global_device_ids=true, to_apply=%region_14.15 | all-reduce | flops 1 | bytes 8 | tf_op jit(solution)/shard_map/psum | solution.py:15
  408.1 12.6 %fusion.60 = f32[4,768,128]{1,2,0:T(8,128)S(1)} fusion(f32[4,768,768]{2,1,0:T(8,128)} %gather_fusion, f32[4,768,128]{1,2,0:T(8,128)S(1)} %broadcast_divide_fusion.2, f32[4,768,128]{1,2,0:T(8,128)S(1)} %copy-done.3), kind=kOutput, calls=%fused_computation.123 | convolution fusion | flops 3625058304 | bytes 14155776 | tf_op jit(solution)/shard_map/bpq,bqc->bpc/dot_general | solution.py:84
  420.7 6.8 multiply_reduce_fusion.11
  428.8 8.3 %psum.264 = f32[2]{0:T(128)S(1)} all-reduce(f32[2]{0:T(128)S(1)} %pad_maximum_fusion.31), channel_id=1, replica_groups=mesh['gx_0'=4,'gx_1'=2,'gy_0'=4,'gy_1'=4] {'gx_0'}, use_global_device_ids=true, to_apply=%region_17.18 | all-reduce | flops 2 | bytes 16 | tf_op jit(solution)/shard_map/psum | solution.py:15
  439.5 7.7 %psum.266 = f32[2]{0:T(128)S(1)} all-reduce(f32[2]{0:T(128)S(1)} %psum.265), channel_id=1, replica_groups=mesh['gx_0'=4,'gx_1'=2,'gy_0'=4,'gy_1'=4] {'gy_0'}, use_global_device_ids=true, to_apply=%region_19.20 | all-reduce | flops 2 | bytes 16 | tf_op jit(solution)/shard_map/psum | solution.py:15
  447.3 9.2 %psum.267 = f32[2]{0:T(128)S(1)} all-reduce(f32[2]{0:T(128)S(1)} %psum.266), channel_id=1, replica_groups=mesh['gx_0'=4,'gx_1'=2,'gy_0'=4,'gy_1'=4] {'gy_1'}, use_global_device_ids=true, to_apply=%region_20.21 | all-reduce | flops 2 | bytes 16 | tf_op jit(solution)/shard_map/psum | solution.py:15
  457.0 5.7 multiply_reduce_fusion.9
  462.8 9.8 %psum.268 = f32[]{:T(128)} all-reduce(f32[]{:T(128)} %get-tuple-element.16), channel_id=1, replica_groups=mesh['gx_0'=4,'gx_1'=2,'gy_0'=4,'gy_1'=4] {'gx_0'}, use_global_device_ids=true, to_apply=%region_22.23 | all-reduce | flops 1 | bytes 8 | tf_op jit(solution)/shard_map/psum | solution.py:15
  475.7 9.8 %psum.270 = f32[]{:T(128)} all-reduce(f32[]{:T(128)} %psum.269), channel_id=1, replica_groups=mesh['gx_0'=4,'gx_1'=2,'gy_0'=4,'gy_1'=4] {'gy_0'}, use_global_device_ids=true, to_apply=%region_24.25 | all-reduce | flops 1 | bytes 8 | tf_op jit(solution)/shard_map/psum | solution.py:15
  485.5 11.6 %psum.271 = f32[]{:T(128)} all-reduce(f32[]{:T(128)} %psum.270), channel_id=1, replica_groups=mesh['gx_0'=4,'gx_1'=2,'gy_0'=4,'gy_1'=4] {'gy_1'}, use_global_device_ids=true, to_apply=%region_25.26 | all-reduce | flops 1 | bytes 8 | tf_op jit(solution)/shard_map/psum | solution.py:15
  506.0 4.4 collective-permute-start.15
  510.4 12.6 %fusion.58 = f32[4,768,128]{1,2,0:T(8,128)S(1)} fusion(f32[4,768,768]{2,1,0:T(8,128)} %gather_fusion, f32[4,768,128]{1,2,0:T(8,128)S(1)} %broadcast_divide_fusion.1, f32[4,768,128]{1,2,0:T(8,128)S(1)} %copy-done.4), kind=kOutput, calls=%fused_computation.117 | convolution fusion | flops 3625058304 | bytes 14155776 | tf_op jit(solution)/shard_map/bpq,bqc->bpc/dot_general | solution.py:84
  523.0 6.9 multiply_reduce_fusion.8
  532.0 8.3 %psum.272 = f32[3]{0:T(128)S(1)} all-reduce(f32[3]{0:T(128)S(1)} %pad_maximum_fusion.32), channel_id=1, replica_groups=mesh['gx_0'=4,'gx_1'=2,'gy_0'=4,'gy_1'=4] {'gx_0'}, use_global_device_ids=true, to_apply=%region_29.30 | all-reduce | flops 3 | bytes 24 | tf_op jit(solution)/shard_map/psum | solution.py:15
  542.7 7.7 %psum.274 = f32[3]{0:T(128)S(1)} all-reduce(f32[3]{0:T(128)S(1)} %psum.273), channel_id=1, replica_groups=mesh['gx_0'=4,'gx_1'=2,'gy_0'=4,'gy_1'=4] {'gy_0'}, use_global_device_ids=true, to_apply=%region_31.32 | all-reduce | flops 3 | bytes 24 | tf_op jit(solution)/shard_map/psum | solution.py:15
  550.5 9.2 %psum.275 = f32[3]{0:T(128)S(1)} all-reduce(f32[3]{0:T(128)S(1)} %psum.274), channel_id=1, replica_groups=mesh['gx_0'=4,'gx_1'=2,'gy_0'=4,'gy_1'=4] {'gy_1'}, use_global_device_ids=true, to_apply=%region_32.33 | all-reduce | flops 3 | bytes 24 | tf_op jit(solution)/shard_map/psum | solution.py:15
  560.3 7.0 multiply_reduce_fusion.5
  567.3 9.8 %psum.276 = f32[]{:T(128)} all-reduce(f32[]{:T(128)} %get-tuple-element.14), channel_id=1, replica_groups=mesh['gx_0'=4,'gx_1'=2,'gy_0'=4,'gy_1'=4] {'gx_0'}, use_global_device_ids=true, to_apply=%region_34.35 | all-reduce | flops 1 | bytes 8 | tf_op jit(solution)/shard_map/psum | solution.py:15
  580.2 9.9 %psum.278 = f32[]{:T(128)} all-reduce(f32[]{:T(128)} %psum.277), channel_id=1, replica_groups=mesh['gx_0'=4,'gx_1'=2,'gy_0'=4,'gy_1'=4] {'gy_0'}, use_global_device_ids=true, to_apply=%region_36.37 | all-reduce | flops 1 | bytes 8 | tf_op jit(solution)/shard_map/psum | solution.py:15
  590.1 11.6 %psum.279 = f32[]{:T(128)} all-reduce(f32[]{:T(128)} %psum.278), channel_id=1, replica_groups=mesh['gx_0'=4,'gx_1'=2,'gy_0'=4,'gy_1'=4] {'gy_1'}, use_global_device_ids=true, to_apply=%region_37.38 | all-reduce | flops 1 | bytes 8 | tf_op jit(solution)/shard_map/psum | solution.py:15
  610.5 4.4 collective-permute-start.19
  614.9 12.6 %fusion.56 = f32[4,768,128]{1,2,0:T(8,128)S(1)} fusion(f32[4,768,768]{2,1,0:T(8,128)} %gather_fusion, f32[4,768,128]{1,2,0:T(8,128)S(1)} %broadcast_divide_fusion, f32[4,768,128]{1,2,0:T(8,128)S(1)} %copy-done.5), kind=kOutput, calls=%fused_computation.110 | convolution fusion | flops 3625058304 | bytes 14155776 | tf_op jit(solution)/shard_map/bpq,bqc->bpc/dot_general | solution.py:84
  627.5 7.0 multiply_reduce_fusion.4
  637.0 8.3 %psum.280 = f32[4]{0:T(128)S(1)} all-reduce(f32[4]{0:T(128)S(1)} %pad_maximum_fusion.33), channel_id=1, replica_groups=mesh['gx_0'=4,'gx_1'=2,'gy_0'=4,'gy_1'=4] {'gx_0'}, use_global_device_ids=true, to_apply=%region_42.43 | all-reduce | flops 4 | bytes 32 | tf_op jit(solution)/shard_map/psum | solution.py:15
  647.8 7.7 %psum.282 = f32[4]{0:T(128)S(1)} all-reduce(f32[4]{0:T(128)S(1)} %psum.281), channel_id=1, replica_groups=mesh['gx_0'=4,'gx_1'=2,'gy_0'=4,'gy_1'=4] {'gy_0'}, use_global_device_ids=true, to_apply=%region_44.45 | all-reduce | flops 4 | bytes 32 | tf_op jit(solution)/shard_map/psum | solution.py:15
  655.5 9.2 %psum.283 = f32[4]{0:T(128)S(1)} all-reduce(f32[4]{0:T(128)S(1)} %psum.282), channel_id=1, replica_groups=mesh['gx_0'=4,'gx_1'=2,'gy_0'=4,'gy_1'=4] {'gy_1'}, use_global_device_ids=true, to_apply=%region_45.46 | all-reduce | flops 4 | bytes 32 | tf_op jit(solution)/shard_map/psum | solution.py:15
  665.3 7.0 multiply_reduce_fusion
  672.3 9.8 %psum.284 = f32[]{:T(128)} all-reduce(f32[]{:T(128)} %multiply_reduce_fusion), channel_id=1, replica_groups=mesh['gx_0'=4,'gx_1'=2,'gy_0'=4,'gy_1'=4] {'gx_0'}, use_global_device_ids=true, to_apply=%region_47.48 | all-reduce | flops 1 | bytes 8 | tf_op jit(solution)/shard_map/psum | solution.py:15
  685.9 9.8 %psum.286 = f32[]{:T(128)} all-reduce(f32[]{:T(128)} %psum.285), channel_id=1, replica_groups=mesh['gx_0'=4,'gx_1'=2,'gy_0'=4,'gy_1'=4] {'gy_0'}, use_global_device_ids=true, to_apply=%region_49.50 | all-reduce | flops 1 | bytes 8 | tf_op jit(solution)/shard_map/psum | solution.py:15
  695.8 11.6 %psum.287 = f32[]{:T(128)} all-reduce(f32[]{:T(128)} %psum.286), channel_id=1, replica_groups=mesh['gx_0'=4,'gx_1'=2,'gy_0'=4,'gy_1'=4] {'gy_1'}, use_global_device_ids=true, to_apply=%region_50.51 | all-reduce | flops 1 | bytes 8 | tf_op jit(solution)/shard_map/psum | solution.py:15
  726.3 5.0 multiply_add_fusion
  (130 shorter events, 100.9 us)
Async XLA Ops:
  0.0 246.9 %copy-start = (f32[768,768]{1,0:T(8,128)S(1)}, f32[768,768]{1,0:T(8,128)}, u32[]{:S(2)}) copy-start(f32[768,768]{1,0:T(8,128)} %param.9) | copy-start | bytes 7077892
  9.9 212.0 %all-to-all-start = ((f32[8,1,768,768]{3,2,1,0:T(8,128)}), f32[8,1,768,768]{3,2,1,0:T(8,128)}, u32[]{:S(2)}, u32[]{:S(2)}) async-start(f32[8,1,768,768]{3,2,1,0:T(8,128)} %stack.65), calls=%async_computation | async-start | bytes 37748736 | tf_op jit(solution)/shard_map/all_to_all | solution.py:79
  20.4 226.5 %collective-permute-start = (f32[1,768,128]{1,2,0:T(8,128)S(1)}, f32[1,768,128]{1,2,0:T(8,128)}, u32[]{:S(2)}, u32[]{:S(2)}) collective-permute-start(f32[1,768,128]{1,2,0:T(8,128)S(1)} %get-tuple-element.37), channel_id=1, source_target_pairs={{16,0},{32,16},{48,32},{64,48},{80,64},{96,80},{112,96},{17,1},{33... | collective-permute-start | bytes 1179656 | tf_op jit(solution)/shard_map/ppermute | solution.py:27
  22.4 224.5 %collective-permute-start.1 = (f32[1,768,128]{1,2,0:T(8,128)S(1)}, f32[1,768,128]{1,2,0:T(8,128)}, u32[]{:S(2)}, u32[]{:S(2)}) collective-permute-start(f32[1,768,128]{1,2,0:T(8,128)S(1)} %get-tuple-element.36), channel_id=1, source_target_pairs={{0,16},{16,32},{32,48},{48,64},{64,80},{80,96},{96,112},{1,17},{17... | collective-permute-start | bytes 1179656 | tf_op jit(solution)/shard_map/ppermute | solution.py:26
  25.7 221.2 %collective-permute-start.2 = (f32[4,768,1]{1,2,0:T(1,128)S(1)}, f32[4,768,1]{1,2,0:T(1,128)S(1)}, u32[]{:S(2)}, u32[]{:S(2)}) collective-permute-start(f32[4,768,1]{1,2,0:T(1,128)S(1)} %get-tuple-element.34), channel_id=1, source_target_pairs={{1,0},{2,1},{3,2},{4,3},{5,4},{6,5},{7,6},{8,7},{9,8},{10,9},{11,1... | collective-permute-start | bytes 36872 | tf_op jit(solution)/shard_map/ppermute | solution.py:27
  27.6 7.2 copy-start.19
  27.7 7.2 copy-start.17
  27.7 219.2 %collective-permute-start.3 = (f32[4,768,1]{1,2,0:T(1,128)S(1)}, f32[4,768,1]{1,2,0:T(1,128)S(1)}, u32[]{:S(2)}, u32[]{:S(2)}) collective-permute-start(f32[4,768,1]{1,2,0:T(1,128)S(1)} %get-tuple-element.35), channel_id=1, source_target_pairs={{0,1},{1,2},{2,3},{3,4},{4,5},{5,6},{6,7},{7,8},{8,9},{9,10},{10,1... | collective-permute-start | bytes 36872 | tf_op jit(solution)/shard_map/ppermute | solution.py:26
  233.2 13.8 %copy-start.1 = (f32[4,768,128]{1,2,0:T(8,128)S(1)}, f32[4,768,128]{1,2,0:T(8,128)}, u32[]{:S(2)}) copy-start(f32[4,768,128]{1,2,0:T(8,128)} %copy.23) | copy-start | bytes 4718596
  233.2 13.8 %copy-start.15 = (f32[4,768,128]{2,1,0:T(8,128)S(1)}, f32[4,768,128]{2,1,0:T(8,128)}, u32[]{:S(2)}) copy-start(f32[4,768,128]{2,1,0:T(8,128)} %param.7) | copy-start | bytes 4718596
  233.2 13.8 %copy-start.16 = (f32[4,768,128]{1,2,0:T(8,128)S(1)}, f32[4,768,128]{1,2,0:T(8,128)}, u32[]{:S(2)}) copy-start(f32[4,768,128]{1,2,0:T(8,128)} %copy.19) | copy-start | bytes 4718596
  233.2 13.8 %copy-start.18 = (f32[768]{0:T(1024)S(1)}, f32[768]{0:T(1024)}, u32[]{:S(2)}) copy-start(f32[768]{0:T(1024)} %param.10) | copy-start | bytes 9220
  295.2 24.0 %copy-start.9 = (f32[4,768,128]{1,2,0:T(8,128)}, f32[4,768,128]{1,2,0:T(8,128)S(1)}, u32[]{:S(2)}) copy-start(f32[4,768,128]{1,2,0:T(8,128)S(1)} %broadcast_divide_fusion.3) | copy-start | bytes 4718596
  295.2 11.4 %copy-start.2 = (f32[4,768,128]{1,2,0:T(8,128)S(1)}, f32[4,768,128]{1,2,0:T(8,128)}, u32[]{:S(2)}) copy-start(f32[4,768,128]{1,2,0:T(8,128)} %copy.23) | copy-start | bytes 4718596
  295.3 23.9 %collective-permute-start.4 = (f32[1,768,128]{1,2,0:T(8,128)S(1)}, f32[1,768,128]{1,2,0:T(8,128)S(1)}, u32[]{:S(2)}, u32[]{:S(2)}) collective-permute-start(f32[1,768,128]{1,2,0:T(8,128)S(1)} %get-tuple-element.33), channel_id=1, source_target_pairs={{16,0},{32,16},{48,32},{64,48},{80,64},{96,80},{112,96},{17,1},{33... | collective-permute-start | bytes 1179656 | tf_op jit(solution)/shard_map/ppermute | solution.py:27
  297.5 21.7 %collective-permute-start.5 = (f32[1,768,128]{1,2,0:T(8,128)S(1)}, f32[1,768,128]{1,2,0:T(8,128)S(1)}, u32[]{:S(2)}, u32[]{:S(2)}) collective-permute-start(f32[1,768,128]{1,2,0:T(8,128)S(1)} %get-tuple-element.32), channel_id=1, source_target_pairs={{0,16},{16,32},{32,48},{48,64},{64,80},{80,96},{96,112},{1,17},{17... | collective-permute-start | bytes 1179656 | tf_op jit(solution)/shard_map/ppermute | solution.py:26
  299.9 19.2 %collective-permute-start.6 = (f32[4,768,1]{1,2,0:T(1,128)S(1)}, f32[4,768,1]{1,2,0:T(1,128)S(1)}, u32[]{:S(2)}, u32[]{:S(2)}) collective-permute-start(f32[4,768,1]{1,2,0:T(1,128)S(1)} %get-tuple-element.30), channel_id=1, source_target_pairs={{1,0},{2,1},{3,2},{4,3},{5,4},{6,5},{7,6},{8,7},{9,8},{10,9},{11,1... | collective-permute-start | bytes 36872 | tf_op jit(solution)/shard_map/ppermute | solution.py:27
  304.7 14.5 %collective-permute-start.7 = (f32[4,768,1]{1,2,0:T(1,128)S(1)}, f32[4,768,1]{1,2,0:T(1,128)S(1)}, u32[]{:S(2)}, u32[]{:S(2)}) collective-permute-start(f32[4,768,1]{1,2,0:T(1,128)S(1)} %get-tuple-element.31), channel_id=1, source_target_pairs={{0,1},{1,2},{2,3},{3,4},{4,5},{5,6},{6,7},{7,8},{8,9},{9,10},{10,1... | collective-permute-start | bytes 36872 | tf_op jit(solution)/shard_map/ppermute | solution.py:26
  397.2 23.5 %copy-start.6 = (f32[4,768,128]{1,2,0:T(8,128)}, f32[4,768,128]{1,2,0:T(8,128)S(1)}, u32[]{:S(2)}) copy-start(f32[4,768,128]{1,2,0:T(8,128)S(1)} %broadcast_divide_fusion.2) | copy-start | bytes 4718596
  397.2 10.9 %copy-start.3 = (f32[4,768,128]{1,2,0:T(8,128)S(1)}, f32[4,768,128]{1,2,0:T(8,128)}, u32[]{:S(2)}) copy-start(f32[4,768,128]{1,2,0:T(8,128)} %copy.23) | copy-start | bytes 4718596
  397.3 23.4 %collective-permute-start.8 = (f32[1,768,128]{1,2,0:T(8,128)S(1)}, f32[1,768,128]{1,2,0:T(8,128)S(1)}, u32[]{:S(2)}, u32[]{:S(2)}) collective-permute-start(f32[1,768,128]{1,2,0:T(8,128)S(1)} %get-tuple-element.29), channel_id=1, source_target_pairs={{16,0},{32,16},{48,32},{64,48},{80,64},{96,80},{112,96},{17,1},{33... | collective-permute-start | bytes 1179656 | tf_op jit(solution)/shard_map/ppermute | solution.py:27
  399.5 21.2 %collective-permute-start.9 = (f32[1,768,128]{1,2,0:T(8,128)S(1)}, f32[1,768,128]{1,2,0:T(8,128)S(1)}, u32[]{:S(2)}, u32[]{:S(2)}) collective-permute-start(f32[1,768,128]{1,2,0:T(8,128)S(1)} %get-tuple-element.28), channel_id=1, source_target_pairs={{0,16},{16,32},{32,48},{48,64},{64,80},{80,96},{96,112},{1,17},{17... | collective-permute-start | bytes 1179656 | tf_op jit(solution)/shard_map/ppermute | solution.py:26
  401.9 18.7 %collective-permute-start.10 = (f32[4,768,1]{1,2,0:T(1,128)S(1)}, f32[4,768,1]{1,2,0:T(1,128)S(1)}, u32[]{:S(2)}, u32[]{:S(2)}) collective-permute-start(f32[4,768,1]{1,2,0:T(1,128)S(1)} %get-tuple-element.26), channel_id=1, source_target_pairs={{1,0},{2,1},{3,2},{4,3},{5,4},{6,5},{7,6},{8,7},{9,8},{10,9},{11,1... | collective-permute-start | bytes 36872 | tf_op jit(solution)/shard_map/ppermute | solution.py:27
  404.0 16.7 %copy-start.10 = (f32[4,768,128]{1,2,0:T(8,128)S(1)}, f32[4,768,128]{1,2,0:T(8,128)}, u32[]{:S(2)}) copy-start(f32[4,768,128]{1,2,0:T(8,128)} %copy-done.9) | copy-start | bytes 4718596
  404.0 16.7 %collective-permute-start.11 = (f32[4,768,1]{1,2,0:T(1,128)S(1)}, f32[4,768,1]{1,2,0:T(1,128)S(1)}, u32[]{:S(2)}, u32[]{:S(2)}) collective-permute-start(f32[4,768,1]{1,2,0:T(1,128)S(1)} %get-tuple-element.27), channel_id=1, source_target_pairs={{0,1},{1,2},{2,3},{3,4},{4,5},{5,6},{6,7},{7,8},{8,9},{9,10},{10,1... | collective-permute-start | bytes 36872 | tf_op jit(solution)/shard_map/ppermute | solution.py:26
  499.3 23.7 %copy-start.13 = (f32[4,768,128]{1,2,0:T(8,128)}, f32[4,768,128]{1,2,0:T(8,128)S(1)}, u32[]{:S(2)}) copy-start(f32[4,768,128]{1,2,0:T(8,128)S(1)} %broadcast_divide_fusion.1) | copy-start | bytes 4718596
  499.3 11.1 %copy-start.4 = (f32[4,768,128]{1,2,0:T(8,128)S(1)}, f32[4,768,128]{1,2,0:T(8,128)}, u32[]{:S(2)}) copy-start(f32[4,768,128]{1,2,0:T(8,128)} %copy.23) | copy-start | bytes 4718596
  499.4 23.6 %collective-permute-start.12 = (f32[1,768,128]{1,2,0:T(8,128)S(1)}, f32[1,768,128]{1,2,0:T(8,128)S(1)}, u32[]{:S(2)}, u32[]{:S(2)}) collective-permute-start(f32[1,768,128]{1,2,0:T(8,128)S(1)} %get-tuple-element.25), channel_id=1, source_target_pairs={{16,0},{32,16},{48,32},{64,48},{80,64},{96,80},{112,96},{17,1},{33... | collective-permute-start | bytes 1179656 | tf_op jit(solution)/shard_map/ppermute | solution.py:27
  501.6 21.4 %collective-permute-start.13 = (f32[1,768,128]{1,2,0:T(8,128)S(1)}, f32[1,768,128]{1,2,0:T(8,128)S(1)}, u32[]{:S(2)}, u32[]{:S(2)}) collective-permute-start(f32[1,768,128]{1,2,0:T(8,128)S(1)} %get-tuple-element.24), channel_id=1, source_target_pairs={{0,16},{16,32},{32,48},{48,64},{64,80},{80,96},{96,112},{1,17},{17... | collective-permute-start | bytes 1179656 | tf_op jit(solution)/shard_map/ppermute | solution.py:26
  504.0 18.9 %collective-permute-start.14 = (f32[4,768,1]{1,2,0:T(1,128)S(1)}, f32[4,768,1]{1,2,0:T(1,128)S(1)}, u32[]{:S(2)}, u32[]{:S(2)}) collective-permute-start(f32[4,768,1]{1,2,0:T(1,128)S(1)} %get-tuple-element.22), channel_id=1, source_target_pairs={{1,0},{2,1},{3,2},{4,3},{5,4},{6,5},{7,6},{8,7},{9,8},{10,9},{11,1... | collective-permute-start | bytes 36872 | tf_op jit(solution)/shard_map/ppermute | solution.py:27
  505.9 17.0 %copy-start.7 = (f32[4,768,128]{1,2,0:T(8,128)S(1)}, f32[4,768,128]{1,2,0:T(8,128)}, u32[]{:S(2)}) copy-start(f32[4,768,128]{1,2,0:T(8,128)} %copy-done.6) | copy-start | bytes 4718596
  506.0 17.0 %copy-start.11 = (f32[4,768,128]{1,2,0:T(8,128)S(1)}, f32[4,768,128]{1,2,0:T(8,128)}, u32[]{:S(2)}) copy-start(f32[4,768,128]{1,2,0:T(8,128)} %copy-done.9) | copy-start | bytes 4718596
  506.0 17.0 %collective-permute-start.15 = (f32[4,768,1]{1,2,0:T(1,128)S(1)}, f32[4,768,1]{1,2,0:T(1,128)S(1)}, u32[]{:S(2)}, u32[]{:S(2)}) collective-permute-start(f32[4,768,1]{1,2,0:T(1,128)S(1)} %get-tuple-element.23), channel_id=1, source_target_pairs={{0,1},{1,2},{2,3},{3,4},{4,5},{5,6},{6,7},{7,8},{8,9},{9,10},{10,1... | collective-permute-start | bytes 36872 | tf_op jit(solution)/shard_map/ppermute | solution.py:26
  603.9 11.0 %copy-start.5 = (f32[4,768,128]{1,2,0:T(8,128)S(1)}, f32[4,768,128]{1,2,0:T(8,128)}, u32[]{:S(2)}) copy-start(f32[4,768,128]{1,2,0:T(8,128)} %copy.23) | copy-start | bytes 4718596
  604.0 23.5 %collective-permute-start.16 = (f32[1,768,128]{1,2,0:T(8,128)S(1)}, f32[1,768,128]{1,2,0:T(8,128)S(1)}, u32[]{:S(2)}, u32[]{:S(2)}) collective-permute-start(f32[1,768,128]{1,2,0:T(8,128)S(1)} %get-tuple-element.21), channel_id=1, source_target_pairs={{16,0},{32,16},{48,32},{64,48},{80,64},{96,80},{112,96},{17,1},{33... | collective-permute-start | bytes 1179656 | tf_op jit(solution)/shard_map/ppermute | solution.py:27
  606.1 21.4 %collective-permute-start.17 = (f32[1,768,128]{1,2,0:T(8,128)S(1)}, f32[1,768,128]{1,2,0:T(8,128)S(1)}, u32[]{:S(2)}, u32[]{:S(2)}) collective-permute-start(f32[1,768,128]{1,2,0:T(8,128)S(1)} %get-tuple-element.20), channel_id=1, source_target_pairs={{0,16},{16,32},{32,48},{48,64},{64,80},{80,96},{96,112},{1,17},{17... | collective-permute-start | bytes 1179656 | tf_op jit(solution)/shard_map/ppermute | solution.py:26
  608.5 19.0 %collective-permute-start.18 = (f32[4,768,1]{1,2,0:T(1,128)S(1)}, f32[4,768,1]{1,2,0:T(1,128)S(1)}, u32[]{:S(2)}, u32[]{:S(2)}) collective-permute-start(f32[4,768,1]{1,2,0:T(1,128)S(1)} %get-tuple-element.18), channel_id=1, source_target_pairs={{1,0},{2,1},{3,2},{4,3},{5,4},{6,5},{7,6},{8,7},{9,8},{10,9},{11,1... | collective-permute-start | bytes 36872 | tf_op jit(solution)/shard_map/ppermute | solution.py:27
  610.4 17.1 %copy-start.8 = (f32[4,768,128]{1,2,0:T(8,128)S(1)}, f32[4,768,128]{1,2,0:T(8,128)}, u32[]{:S(2)}) copy-start(f32[4,768,128]{1,2,0:T(8,128)} %copy-done.6) | copy-start | bytes 4718596
  610.4 17.1 %copy-start.12 = (f32[4,768,128]{1,2,0:T(8,128)S(1)}, f32[4,768,128]{1,2,0:T(8,128)}, u32[]{:S(2)}) copy-start(f32[4,768,128]{1,2,0:T(8,128)} %copy-done.9) | copy-start | bytes 4718596
  610.5 17.1 %copy-start.14 = (f32[4,768,128]{1,2,0:T(8,128)S(1)}, f32[4,768,128]{1,2,0:T(8,128)}, u32[]{:S(2)}) copy-start(f32[4,768,128]{1,2,0:T(8,128)} %copy-done.13) | copy-start | bytes 4718596
  610.5 17.0 %collective-permute-start.19 = (f32[4,768,1]{1,2,0:T(1,128)S(1)}, f32[4,768,1]{1,2,0:T(1,128)S(1)}, u32[]{:S(2)}, u32[]{:S(2)}) collective-permute-start(f32[4,768,1]{1,2,0:T(1,128)S(1)} %get-tuple-element.19), channel_id=1, source_target_pairs={{0,1},{1,2},{2,3},{3,4},{4,5},{5,6},{6,7},{7,8},{8,9},{9,10},{10,1... | collective-permute-start | bytes 36872 | tf_op jit(solution)/shard_map/ppermute | solution.py:26
